TPU v7x, 256 devices: a 8x8x2 block of a 8x8x16 slice. The times are simulated.
256 devices in a mesh: groups: 2 (over z), seq: 16 (over x, core), qset: 8 (over y).
Axes of the slice: x: 8, y: 8, z: 2, core: 2. Of those that a mesh axis runs over, the one named last changes fastest.
The devices are a block of a 8x8x16 slice.
Arguments:
- states: bfloat16 [16, 16, 128, 4096], P(('groups', 'qset'), 'seq'), parts along dimension 0, may hold values from -7 to 7
- enc_gain: bfloat16 [4096], replicated, may hold values from 0.25 to 1.75
- dec_states: bfloat16 [32, 64, 4096], P(('groups', 'qset')), parts along dimension 0, may hold values from -7 to 7
- dec_gain: bfloat16 [4096], replicated, may hold values from 0.25 to 1.75
- query_weight: bfloat16 [4096, 4096], P(None, 'seq'), may hold values from -0.375 to 0.375
- key_value_weight: bfloat16 [4096, 2, 4096], P(None, None, 'seq'), may hold values from -0.0625 to 0.0625
- out_weight: bfloat16 [4096, 4096], P('seq'), may hold values from -0.75 to 0.75
- question_of: int32 [16, 16, 1], P('groups'), parts along dimension 0, may hold values from 0 to 15; in each aligned block of 16 rows (0 to 15, 16 to 31, ..., all dimensions but the last counted through in order) at most 2 rows name the same one
Outputs:
- mixed: bfloat16 [32, 64, 4096], P(('groups', 'qset'), None, 'seq'), parts along dimension 0
There are 2 independent parts, one for each index of `groups`. A program takes and returns all parts, laid end to end along the dimension named above; an argument that names none is the same for every part. Nothing has to cross between parts.
Inputs may be any that keep to these rules, and one draw needn't show every extreme that they name: `question_of`: within each index of the first dimension (one source group of 16 passages) at most 2 passages name the same question, and exactly 2 do for some question in some groups; every question is named by at least one passage.
All inputs are finite; a program needn't handle non-finite values.
Results may differ from a plain program's by a relative error of at most 0.014.
The roundings to bfloat16 on the way count: a program that leaves them out, or rounds other values in their place, can miss the bound.
Values may be sent and summed in bfloat16 or wider, within the bound.
A program may use at most 128 MiB of HBM per device.

v0:
```python
import math
import jax
import jax.numpy as jnp
from jax import lax
from jax.sharding import PartitionSpec as P

HD = 64
CAP = 2
EPSILON = 1e-06
MASKED_SCORE = -1e30


def from_everyone(shard, axis):
    devices = lax.axis_size(axis)
    return lax.all_to_all(
        jnp.broadcast_to(shard[None], (devices, *shard.shape)), axis, 0, 0, tiled=True
    )


def laid_out(pieces, dim):
    dims = list(pieces.shape[1:])
    dims[dim] *= pieces.shape[0]
    return jnp.moveaxis(pieces, 0, dim).reshape(dims)


def gather_directly(shard, axis, dim):
    pieces = from_everyone(shard, axis)
    return laid_out(pieces, dim)


def over_copies(shard, axis):
    return from_everyone(shard, axis).max(axis=0)


def split_up(shard, dim, devices):
    dims = shard.shape
    pieces = shard.reshape(*dims[:dim], devices, dims[dim] // devices, *dims[dim + 1 :])
    return jnp.moveaxis(pieces, dim, 0)


def sent_and_summed(shard, axis, dim):
    pieces = split_up(shard, dim, lax.axis_size(axis))
    arrived = lax.all_to_all(pieces, axis, split_axis=0, concat_axis=0, tiled=True)
    return arrived.astype(jnp.float32).sum(axis=0)


def sent_together(arrays, axis, dim, along):
    widths = [math.prod(a.shape[along:]) for a in arrays]
    both = jnp.concatenate(
        [a.reshape(*a.shape[:along], w) for a, w in zip(arrays, widths)], axis=along
    )
    result = sent_and_summed(both, axis, dim)
    pieces = jnp.split(result, [sum(widths[:k]) for k in range(1, len(widths))], axis=along)
    return tuple(
        (b.reshape(*result.shape[:along], *a.shape[along:]) for a, b in zip(arrays, pieces))
    )


def scaled_norm(rows_in, gain_vec):
    rows_f32 = rows_in.astype(jnp.float32)
    mean_square = jnp.mean(rows_f32 * rows_f32, axis=-1, keepdims=True)
    return rows_f32 * lax.rsqrt(mean_square + EPSILON) * gain_vec.astype(jnp.float32)


def body(
    states, enc_gain, dec_states, dec_gain, query_weight, key_value_weight, out_weight, question_of
):
    model_width = states.shape[-1]
    passage_len = states.shape[2]
    group_count = lax.axis_size("qset")
    shard_count = lax.axis_size("seq")
    group_index = lax.axis_index("qset")
    shard_index = lax.axis_index("seq")
    local_questions = dec_states.shape[0]
    dec_len = dec_states.shape[1]
    head_cols = query_weight.shape[1]
    heads_here = head_cols // HD
    all_questions = local_questions * group_count
    kv_weight = key_value_weight.reshape(model_width, 2 * head_cols)
    own_rows = scaled_norm(states[0, 0], enc_gain).astype(jnp.bfloat16)[None]
    gathered_rows = lax.all_gather(own_rows, "seq", axis=0, tiled=True)
    piece_count = gathered_rows.shape[0]
    flat_rows = gathered_rows.reshape(piece_count * passage_len, model_width)
    product = jnp.dot(flat_rows, kv_weight, preferred_element_type=jnp.float32)
    key_vals = product.astype(jnp.bfloat16).reshape(piece_count, passage_len, 2 * head_cols)
    passage_table = question_of[:, :, 0]
    numbers = jnp.arange(all_questions, dtype=jnp.int32)
    counts = jnp.sum(
        (passage_table[:, :, None] == numbers[None, None, :]).astype(jnp.int32), axis=1
    )
    group_table = lax.dynamic_index_in_dim(passage_table, group_index, 0, keepdims=False)
    matches = (group_table[:, None] == numbers[None, :]).astype(jnp.int32)
    earlier = jnp.cumsum(matches, axis=0) - matches
    slot_rank = jnp.sum(earlier * matches, axis=1)
    slot_index = group_table * CAP + slot_rank
    picker = (
        jnp.arange(all_questions * CAP, dtype=jnp.int32)[:, None] == slot_index[None, :]
    ).astype(jnp.bfloat16)
    packed = jnp.einsum("as,spc->apc", picker, key_vals, preferred_element_type=jnp.float32).astype(
        jnp.bfloat16
    )
    dec_rows = (
        scaled_norm(dec_states, dec_gain)
        .astype(jnp.bfloat16)
        .reshape(local_questions * dec_len, model_width)
    )
    queries = jnp.dot(dec_rows, query_weight, preferred_element_type=jnp.float32)
    queries = queries.astype(jnp.bfloat16).reshape(local_questions, dec_len, heads_here, HD)
    slot_numbers = jnp.arange(CAP, dtype=jnp.int32)
    gathered = gather_directly(queries, "qset", 0)
    local_keys = packed.reshape(all_questions, CAP * passage_len, 2 * head_cols)
    key_rows = local_keys[:, :, :head_cols].reshape(all_questions, -1, heads_here, HD)
    value_rows = local_keys[:, :, head_cols:].reshape(all_questions, -1, heads_here, HD)
    own_counts = lax.dynamic_index_in_dim(counts, group_index, 0, keepdims=False)
    live_slots = own_counts[:, None] > slot_numbers[None, :]
    live_rows = jnp.broadcast_to(live_slots[:, :, None], (all_questions, CAP, passage_len)).reshape(
        all_questions, -1
    )
    scores = jnp.einsum("qthd,qrhd->qhtr", gathered, key_rows, preferred_element_type=jnp.float32)
    scores = jnp.where(live_rows[:, None, None, :], scores, MASKED_SCORE)
    row_peak = over_copies(jnp.max(scores, axis=-1), "qset")
    weights = jnp.where(live_rows[:, None, None, :], jnp.exp(scores - row_peak[..., None]), 0.0)
    group_total = jnp.sum(weights, axis=-1)
    group_summed = jnp.einsum(
        "qhtr,qrhd->qthd",
        weights.astype(jnp.bfloat16),
        value_rows,
        preferred_element_type=jnp.float32,
    )
    summed, row_total = sent_together(
        (group_summed.astype(jnp.bfloat16), group_total.astype(jnp.bfloat16)), "qset", 0, 1
    )
    attended = summed / jnp.transpose(row_total, (0, 2, 1))[..., None]
    attended = attended.astype(jnp.bfloat16).reshape(local_questions * dec_len, head_cols)
    piece_cols = model_width // shard_count
    residual = lax.dynamic_slice_in_dim(dec_states, shard_index * piece_cols, piece_cols, 2).astype(
        jnp.float32
    )
    owned_rows = sent_and_summed(
        lax.dot_general(
            out_weight, attended, (((0,), (1,)), ((), ())), preferred_element_type=jnp.float32
        ).astype(jnp.bfloat16),
        "seq",
        0,
    )
    owned_sum = jnp.transpose(owned_rows).reshape(local_questions, dec_len, piece_cols)
    return (residual + owned_sum).astype(jnp.bfloat16)


def solution(mesh):
    return jax.shard_map(
        body,
        mesh=mesh,
        in_specs=(
            P(("groups", "qset"), "seq", None, None),
            P(),
            P(("groups", "qset"), None, None),
            P(),
            P(None, "seq"),
            P(None, None, "seq"),
            P("seq", None),
            P("groups", None, None),
        ),
        out_specs=P(("groups", "qset"), None, "seq"),
        check_vma=False,
    )
```

profile of v0, /device:TPU:513, one launch (start us, length us, event | category | flops | bytes accessed | tf_op | source)
XLA Modules:
  0.0 255.8 jit_solution(8536282614529816746)
XLA Ops:
  6.5 0.0 copy-start
  6.6 0.0 all-gather.2.cloned.1.call-start
  6.6 0.8 convert_element_type.98
  7.4 0.0 copy-start.4
  7.4 1.6 fusion.8
  9.0 2.6 %fusion.7 = bf16[1,128,4096]{2,1,0:T(8,128)(2,1)} fusion(bf16[1,1,128,4096]{3,2,1,0:T(8,128)(2,1)} %param.8, f32[4096]{0:T(1024)S(1)} %convert_element_type.98, f32[128]{0:T(128)S(1)} %add_rsqrt_fusion.1), kind=kLoop, calls=%fused_computation.16 | loop fusion | flops 2097152 | bytes 2114048 | tf_op jit(solution)/shard_map/convert_element_type | solution.py:80
  11.6 0.1 all-gather.2.cloned.1.call-update
  11.7 0.0 copy-done.4
  11.7 0.0 copy-start.3
  11.7 0.0 copy-done.2
  11.7 0.3 fusion.2
  12.0 0.3 fusion.4
  12.3 0.9 copy-done.3
  13.3 0.4 convolution_convert_fusion.3
  13.7 0.0 copy-start.5
  13.7 0.1 broadcast_in_dim.31
  13.9 1.2 broadcast_bitcast_fusion
  15.1 3.0 %reshape.185 = bf16[8,2,16384]{2,1,0:T(2,128)(2,1)} reshape(bf16[8,2,4,64,64]{4,3,2,1,0:T(8,128)(2,1)} %broadcast_bitcast_fusion) | data formatting | bytes 1048576
  18.1 13.7 %all-to-all-start = ((bf16[8,2,16384]{2,1,0:T(2,128)(2,1)}), bf16[8,2,16384]{2,1,0:T(2,128)(2,1)}, u32[]{:S(2)}, u32[]{:S(2)}) async-start(bf16[8,2,16384]{2,1,0:T(2,128)(2,1)} %reshape.185), calls=%async_computation | async-start | bytes 1048576 | tf_op jit(solution)/shard_map/all_to_all | solution.py:15
  31.8 0.0 copy-done.5
  31.8 0.1 fusion.22
  31.9 4.8 %copy.47 = bf16[512,8,2,256]{3,1,2,0:T(8,128)(2,1)} copy(bf16[512,8,2,256]{3,2,1,0:T(2,128)(2,1)} %bitcast.61) | data formatting | bytes 8388608
  36.8 0.1 convert_reduce_fusion.2
  36.9 0.1 iota_compare_fusion.1
  37.0 0.1 broadcast_in_dim.28
  37.1 0.2 select_reduce_fusion.1
  37.3 6.8 %all-to-all-done = bf16[8,2,16384]{2,1,0:T(2,128)(2,1)} async-done(((bf16[8,2,16384]{2,1,0:T(2,128)(2,1)}), bf16[8,2,16384]{2,1,0:T(2,128)(2,1)}, u32[]{:S(2)}, u32[]{:S(2)}) %all-to-all-start) | async-done | bytes 524320 | tf_op jit(solution)/shard_map/all_to_all | solution.py:15
  44.1 3.1 %reshape.186 = bf16[8,2,4,64,64]{4,3,2,1,0:T(8,128)(2,1)} reshape(bf16[8,2,16384]{2,1,0:T(2,128)(2,1)} %all-to-all-done) | data formatting | bytes 1048576
  47.1 80.0 %all-gather.2.cloned.1.call-done = bf16[16,128,4096]{2,1,0:T(8,128)(2,1)} async-done(((bf16[1,128,4096]{2,1,0:T(8,128)(2,1)}), bf16[16,128,4096]{2,1,0:T(8,128)(2,1)}) %all-gather.2.cloned.1.call-update) | async-done | bytes 16777232 | tf_op jit(solution)/shard_map/all_gather | solution.py:81
  127.2 13.6 %convolution_convert_fusion.1 = bf16[2048,512]{1,0:T(8,128)(2,1)S(1)} fusion(bf16[2048,4096]{1,0:T(8,128)(2,1)} %bitcast.74, bf16[4096,512]{1,0:T(8,128)(2,1)} %bitcast.62), kind=kOutput, calls=%fused_computation.5 | convolution fusion | flops 8590983168 | bytes 23068672 | tf_op jit(solution)/shard_map/dot_general | solution.py:84
  140.8 1.6 convolution_convert_fusion.2
  142.4 2.4 copy.37
  144.8 2.5 fusion.30
  147.3 3.9 %copy.40 = bf16[16,256,256]{1,2,0:T(8,128)(2,1)} copy(bf16[16,256,256]{2,1,0:T(8,128)(2,1)} %get-tuple-element.6) | data formatting | bytes 4194304 | tf_op jit(solution)/shard_map/slice | solution.py:112
  151.2 4.5 %select_reduce_fusion = (f32[16,4,64]{2,1,0:T(4,128)S(1)}, f32[16,4,64,256]{3,2,1,0:T(8,128)}) fusion(pred[16,256]{1,0:T(8,128)(4,1)S(1)} %bitcast.68, bf16[16,64,4,64]{3,1,2,0:T(8,128)(2,1)} %bitcast.59, bf16[16,256,4,64]{1,3,2,0:T(8,128)(2,1)} %bitcast.58), kind=kOutput, calls=%fused_computation.2 | convolution fusion | flops 136310784 | bytes 6836224 | tf_op jit(solution)/shard_map/qthd,qrhd->qhtr/dot_general | solution.py:119
  155.8 0.8 reshape.187
  156.6 6.7 %all-to-all-start.1 = ((f32[8,1,4096]{2,1,0:T(1,128)}), f32[8,1,4096]{2,1,0:T(1,128)S(1)}, u32[]{:S(2)}, u32[]{:S(2)}) async-start(f32[8,1,4096]{2,1,0:T(1,128)} %reshape.187), calls=%async_computation.1 | async-start | bytes 262144 | tf_op jit(solution)/shard_map/all_to_all | solution.py:15
  163.3 3.9 %copy.38 = bf16[16,256,256]{1,2,0:T(8,128)(2,1)} copy(bf16[16,256,256]{2,1,0:T(8,128)(2,1)} %get-tuple-element.5) | data formatting | bytes 4194304 | tf_op jit(solution)/shard_map/slice | solution.py:113
  167.2 4.2 %all-to-all-done.1 = f32[8,1,4096]{2,1,0:T(1,128)S(1)} async-done(((f32[8,1,4096]{2,1,0:T(1,128)}), f32[8,1,4096]{2,1,0:T(1,128)S(1)}, u32[]{:S(2)}, u32[]{:S(2)}) %all-to-all-start.1) | async-done | bytes 131104 | tf_op jit(solution)/shard_map/all_to_all | solution.py:15
  171.5 0.5 broadcast.92
  172.0 1.0 reduce.1
  172.9 0.1 reshape.188
  173.1 0.0 copy-start.1
  173.1 3.3 %fusion = bf16[16,4,64]{2,1,0:T(4,128)(2,1)S(1)} fusion(f32[16,4,64,256]{3,2,1,0:T(8,128)} %get-tuple-element.8, f32[16,4,64]{2,1,0:T(4,128)S(1)} %copy.42, pred[16,256]{1,0:T(8,128)(4,1)S(1)} %bitcast.69), kind=kLoop, calls=%fused_computation.3 | loop fusion | flops 4190208 | bytes 4222976 | tf_op jit(solution)/shard_map/reduce_sum | solution.py:123
  176.4 0.2 copy-done.1
  176.5 3.5 %fusion.19 = bf16[16,64,4,64]{1,3,2,0:T(8,128)(2,1)} fusion(bf16[16,256,4,64]{1,3,2,0:T(8,128)(2,1)} %bitcast.66, f32[16,4,64,256]{3,2,1,0:T(8,128)S(1)} %copy-done.1, f32[16,4,64]{2,1,0:T(4,128)S(1)} %copy.42, pred[16,256]{1,0:T(8,128)(4,1)S(1)} %bitcast.70), kind=kOutput, calls=%fused_computation.26 | convolution fusion | flops 138674176 | bytes 6836224 | tf_op jit(solution)/shard_map/qhtr,qrhd->qthd/dot_general | solution.py:124
  180.0 2.4 copy.43
  182.4 3.3 %concatenate.6 = bf16[8,2,16384]{2,1,0:T(2,128)(2,1)} reshape(bf16[16,64,4,64]{3,2,1,0:T(4,128)(2,1)} %copy.43) | data formatting | bytes 1048576 | tf_op jit(solution)/shard_map/concatenate | solution.py:49
  185.8 0.1 convert_element_type.111
  185.9 1.5 pad_maximum_fusion
  187.4 17.2 %all_to_all.20 = bf16[8,2,16640]{2,1,0:T(2,128)(2,1)S(1)} all-to-all(bf16[8,2,16640]{2,1,0:T(2,128)(2,1)S(1)} %pad_maximum_fusion), channel_id=1, replica_groups=mesh['groups'=2,'seq'=16,'qset'=8] {'qset'}, dimensions={0} | all-to-all | bytes 1064960 | tf_op jit(solution)/shard_map/all_to_all | solution.py:43
  204.6 0.5 convert_reduce_fusion.1
  205.1 0.1 reshape.180
  205.2 0.7 copy.44
  206.0 1.0 div.27
  207.0 0.8 div.28
  207.8 0.1 reshape.179
  208.0 0.0 copy-done
  208.0 1.4 convolution_convert_fusion
  209.3 1.1 copy.53
  210.5 8.4 %all-to-all-start.3 = ((bf16[16,256,128]{1,2,0:T(8,128)(2,1)}), bf16[16,256,128]{1,2,0:T(8,128)(2,1)}, u32[]{:S(2)}, u32[]{:S(2)}) async-start(bf16[16,256,128]{1,2,0:T(8,128)(2,1)} %bitcast.63), calls=%async_computation.3 | async-start | bytes 2097152 | tf_op jit(solution)/shard_map/all_to_all | solution.py:43
  218.8 28.1 %all-to-all-done.3 = bf16[16,256,128]{1,2,0:T(8,128)(2,1)} async-done(((bf16[16,256,128]{1,2,0:T(8,128)(2,1)}), bf16[16,256,128]{1,2,0:T(8,128)(2,1)}, u32[]{:S(2)}, u32[]{:S(2)}) %all-to-all-start.3) | async-done | bytes 1048608 | tf_op jit(solution)/shard_map/all_to_all | solution.py:43
  246.9 1.4 convert_reduce_fusion
  248.3 0.7 add_convert_fusion
  (16 shorter events, 0.2 us)
Async XLA Ops:
  6.5 201.4 %copy-start = (bf16[256,4096]{1,0:T(8,128)(2,1)S(1)}, bf16[256,4096]{1,0:T(8,128)(2,1)}, u32[]{:S(2)}) copy-start(bf16[256,4096]{1,0:T(8,128)(2,1)} %param.14) | copy-start | bytes 6291460
  6.6 120.6 %all-gather.2.cloned.1.call-start = ((), (), s32[]{:S(2)}) async-start(), calls=%async_computation.4 | async-start | bytes 17825792 | tf_op jit(solution)/shard_map/all_gather | solution.py:81
  7.4 4.3 %copy-start.4 = (bf16[4096]{0:T(1024)(128)(2,1)S(1)}, bf16[4096]{0:T(1024)(128)(2,1)}, u32[]{:S(2)}) copy-start(bf16[4096]{0:T(1024)(128)(2,1)} %param.11) | copy-start | bytes 24580
  7.4 4.3 %copy-start.2 = (bf16[2,64,4096]{2,1,0:T(8,128)(2,1)S(1)}, bf16[2,64,4096]{2,1,0:T(8,128)(2,1)}, u32[]{:S(2)}) copy-start(bf16[2,64,4096]{2,1,0:T(8,128)(2,1)} %param.10) | copy-start | bytes 3145732
  11.7 1.6 copy-start.3
  13.7 18.1 %copy-start.5 = (s32[8,16,1]{1,2,0:T(1,128)S(1)}, s32[8,16,1]{1,2,0:T(1,128)}, u32[]{:S(2)}) copy-start(s32[8,16,1]{1,2,0:T(1,128)} %param.15) | copy-start | bytes 1540
  18.1 25.9 %all-to-all-start = ((bf16[8,2,16384]{2,1,0:T(2,128)(2,1)}), bf16[8,2,16384]{2,1,0:T(2,128)(2,1)}, u32[]{:S(2)}, u32[]{:S(2)}) async-start(bf16[8,2,16384]{2,1,0:T(2,128)(2,1)} %reshape.185), calls=%async_computation | async-start | bytes 1048576 | tf_op jit(solution)/shard_map/all_to_all | solution.py:15
  156.6 14.9 %all-to-all-start.1 = ((f32[8,1,4096]{2,1,0:T(1,128)}), f32[8,1,4096]{2,1,0:T(1,128)S(1)}, u32[]{:S(2)}, u32[]{:S(2)}) async-start(f32[8,1,4096]{2,1,0:T(1,128)} %reshape.187), calls=%async_computation.1 | async-start | bytes 262144 | tf_op jit(solution)/shard_map/all_to_all | solution.py:15
  173.1 3.5 %copy-start.1 = (f32[16,4,64,256]{3,2,1,0:T(8,128)S(1)}, f32[16,4,64,256]{3,2,1,0:T(8,128)}, u32[]{:S(2)}) copy-start(f32[16,4,64,256]{3,2,1,0:T(8,128)} %get-tuple-element.8) | copy-start | bytes 12582916
  210.5 36.5 %all-to-all-start.3 = ((bf16[16,256,128]{1,2,0:T(8,128)(2,1)}), bf16[16,256,128]{1,2,0:T(8,128)(2,1)}, u32[]{:S(2)}, u32[]{:S(2)}) async-start(bf16[16,256,128]{1,2,0:T(8,128)(2,1)} %bitcast.63), calls=%async_computation.3 | async-start | bytes 2097152 | tf_op jit(solution)/shard_map/all_to_all | solution.py:43
Sparse Core Ops, SparseCore 0:
  11.8 115.3 all-gather.1
where the time goes:
time: 257 us; the launch traced here: 256 us
  waiting for transfers between devices  119 us (46%)
  local copies, waits for them, and re-layouts  37.5 us (15%)
  starting transfers between devices  28.8 us (11%)
  matrix products  25 us (10%)
  blocking collectives  17.2 us (7%)
  other arithmetic  14.4 us (6%)
  between operations  13.7 us (5%)
    all_gather x1, waiting for transfers between devices, body(): gathered_rows = lax.all_gather(own_rows, 'seq', axis=0, tiled=True)  80 us
    all_to_all x1, waiting for transfers between devices, sent_and_summed(): lax.all_to_all(pieces, axis, split_axis=0, concat_axis=0, tiled=True)  28.1 us
    all_to_all x2, starting transfers between devices, from_everyone(): lax.all_to_all(jnp.broadcast_to(shard[None], (devices, *shard.shape)), ax...  20.4 us
    all_to_all x1, blocking collectives, sent_and_summed(): lax.all_to_all(pieces, axis, split_axis=0, concat_axis=0, tiled=True)  17.2 us
    unnamed x20, local copies, waits for them, and re-layouts  14.2 us
    dot_general x1, matrix products, body(): product = jnp.dot(flat_rows, kv_weight, preferred_element_type=jnp.float32)  13.6 us
    all_to_all x2, waiting for transfers between devices, from_everyone(): lax.all_to_all(jnp.broadcast_to(shard[None], (devices, *shard.shape)), ax...  11 us
    all_to_all x1, starting transfers between devices, sent_and_summed(): lax.all_to_all(pieces, axis, split_axis=0, concat_axis=0, tiled=True)  8.36 us
  transfers between devices with their start and end apart: 4, of which 4 were waited for; matrix products, arithmetic and copies ran while one was open for 7% of the time, Pallas kernels for 0%

commit v1 on v0

--- a/solution.py
+++ b/solution.py
@@ -78,7 +78,9 @@
     all_questions = local_questions * group_count
     kv_weight = key_value_weight.reshape(model_width, 2 * head_cols)
     own_rows = scaled_norm(states[0, 0], enc_gain).astype(jnp.bfloat16)[None]
-    gathered_rows = lax.all_gather(own_rows, "seq", axis=0, tiled=True)
+    gathered_rows = jnp.concatenate(
+        lax.all_to_all(jnp.stack([own_rows] * lax.axis_size("seq")), "seq", 0, 0), axis=0
+    )
     piece_count = gathered_rows.shape[0]
     flat_rows = gathered_rows.reshape(piece_count * passage_len, model_width)
     product = jnp.dot(flat_rows, kv_weight, preferred_element_type=jnp.float32)

time: 257 us -> 535 us (2.08)
  waiting for transfers between devices: 119 us -> 397 us
  starting transfers between devices: 28.8 us -> 44.2 us
  between operations: 13.7 us -> 0.28 us
    all_to_all x0 -> x1, waiting for transfers between devices: none -> 356 us  [body(): lax.all_to_all(jnp.stack([own_rows] * lax.axis_size('seq')), 'seq', 0, 0)]
    all_gather x1 -> x0, waiting for transfers between devices: 80 us -> none  [body(): gathered_rows = lax.all_gather(own_rows, 'seq', axis=0, tiled=True)]
    all_to_all x0 -> x1, starting transfers between devices: none -> 17 us  [body(): lax.all_to_all(jnp.stack([own_rows] * lax.axis_size('seq')), 'seq', 0, 0)]
    another operation x0 -> x1, local copies, waits for them, and re-layouts: none -> 5.92 us  [body(): jnp.stack([own_rows] * lax.axis_size('seq'))]
  transfers between devices with their start and end apart: 4 -> 4, of which waited for: 4 -> 4; matrix products, arithmetic and copies ran while one was open for 7% -> 3% of each run, Pallas kernels for 0% -> 0%
where the time goes in v1:
time: 535 us; the launch traced here: 534 us
  waiting for transfers between devices  397 us (74%)
  starting transfers between devices  44.2 us (8%)
  local copies, waits for them, and re-layouts  37.2 us (7%)
  matrix products  23.8 us (4%)
  blocking collectives  17.4 us (3%)
  other arithmetic  14.2 us (3%)
    all_to_all x1, waiting for transfers between devices, body(): lax.all_to_all(jnp.stack([own_rows] * lax.axis_size('seq')), 'seq', 0, 0)  356 us
    all_to_all x1, waiting for transfers between devices, sent_and_summed(): lax.all_to_all(pieces, axis, split_axis=0, concat_axis=0, tiled=True)  28 us
    all_to_all x2, starting transfers between devices, from_everyone(): lax.all_to_all(jnp.broadcast_to(shard[None], (devices, *shard.shape)), ax...  17.5 us
    all_to_all x1, blocking collectives, sent_and_summed(): lax.all_to_all(pieces, axis, split_axis=0, concat_axis=0, tiled=True)  17.4 us
    all_to_all x1, starting transfers between devices, body(): lax.all_to_all(jnp.stack([own_rows] * lax.axis_size('seq')), 'seq', 0, 0)  17 us
    all_to_all x2, waiting for transfers between devices, from_everyone(): lax.all_to_all(jnp.broadcast_to(shard[None], (devices, *shard.shape)), ax...  13.7 us
    dot_general x1, matrix products, body(): product = jnp.dot(flat_rows, kv_weight, preferred_element_type=jnp.float32)  13.6 us
    unnamed x20, local copies, waits for them, and re-layouts  12.7 us
  transfers between devices with their start and end apart: 4, of which 4 were waited for; matrix products, arithmetic and copies ran while one was open for 3% of the time, Pallas kernels for 0%

profile of v1, /device:TPU:513, one launch (start us, length us, event | category | flops | bytes accessed | tf_op | source)
XLA Modules:
  0.0 534.4 jit_solution(2680741458143424060)
XLA Ops:
  0.0 0.0 copy-start
  0.0 0.0 copy-start.3
  0.0 0.9 convert_element_type.85
  0.9 1.6 fusion.5
  2.5 1.6 fusion.7
  4.1 0.0 copy-done.3
  4.1 0.4 convolution_convert_fusion.3
  4.5 0.0 copy-start.4
  4.5 0.0 copy-start.2
  4.5 0.1 broadcast_in_dim.31
  4.7 1.2 broadcast_bitcast_fusion
  5.9 3.0 reshape.135
  9.0 13.7 %all-to-all-start.1 = ((bf16[8,2,16384]{2,1,0:T(2,128)(2,1)}), bf16[8,2,16384]{2,1,0:T(2,128)(2,1)}, u32[]{:S(2)}, u32[]{:S(2)}) async-start(bf16[8,2,16384]{2,1,0:T(2,128)(2,1)} %reshape.135), calls=%async_computation.1 | async-start | bytes 1048576 | tf_op jit(solution)/shard_map/all_to_all | solution.py:15
  22.7 0.0 copy-done.4
  22.7 0.0 copy-done.2
  22.7 0.3 fusion.2
  23.0 1.6 fusion.21
  24.5 10.4 %all-to-all-done.1 = bf16[8,2,16384]{2,1,0:T(2,128)(2,1)} async-done(((bf16[8,2,16384]{2,1,0:T(2,128)(2,1)}), bf16[8,2,16384]{2,1,0:T(2,128)(2,1)}, u32[]{:S(2)}, u32[]{:S(2)}) %all-to-all-start.1) | async-done | bytes 524320 | tf_op jit(solution)/shard_map/all_to_all | solution.py:15
  34.9 5.9 %stack.3 = bf16[16,1,128,4096]{3,2,1,0:T(8,128)(2,1)} broadcast(bf16[128,4096]{1,0:T(8,128)(2,1)S(1)} %fusion.21), dimensions={2,3} | broadcast | bytes 17825792 | tf_op jit(solution)/shard_map/stack | solution.py:82
  40.8 17.0 %all-to-all-start = ((bf16[16,1,128,4096]{3,2,1,0:T(8,128)(2,1)}), bf16[16,1,128,4096]{3,2,1,0:T(8,128)(2,1)}, u32[]{:S(2)}, u32[]{:S(2)}) async-start(bf16[16,1,128,4096]{3,2,1,0:T(8,128)(2,1)} %stack.3), calls=%async_computation | async-start | bytes 33554432 | tf_op jit(solution)/shard_map/all_to_all | solution.py:82
  57.8 0.0 copy-done.5
  57.8 0.1 fusion.22
  57.9 5.0 copy.47
  62.9 0.1 convert_reduce_fusion.2
  63.0 0.1 iota_compare_fusion.1
  63.1 0.1 broadcast_in_dim.28
  63.2 0.2 select_reduce_fusion.1
  63.4 2.3 reshape.136
  65.7 355.6 %all-to-all-done = bf16[16,1,128,4096]{3,2,1,0:T(8,128)(2,1)} async-done(((bf16[16,1,128,4096]{3,2,1,0:T(8,128)(2,1)}), bf16[16,1,128,4096]{3,2,1,0:T(8,128)(2,1)}, u32[]{:S(2)}, u32[]{:S(2)}) %all-to-all-start) | async-done | bytes 16777248 | tf_op jit(solution)/shard_map/all_to_all | solution.py:82
  421.3 13.6 %convolution_convert_fusion.1 = bf16[2048,512]{1,0:T(8,128)(2,1)S(1)} fusion(bf16[2048,4096]{1,0:T(8,128)(2,1)} %bitcast.3, bf16[4096,512]{1,0:T(8,128)(2,1)} %bitcast.56), kind=kOutput, calls=%fused_computation.5 | convolution fusion | flops 8590983168 | bytes 23068672 | tf_op jit(solution)/shard_map/dot_general | solution.py:86
  434.8 1.6 convolution_convert_fusion.2
  436.4 2.4 copy.37
  438.8 2.5 fusion.30
  441.3 3.9 copy.40
  445.2 4.2 select_reduce_fusion
  449.5 0.8 reshape.137
  450.3 3.8 all-to-all-start.2
  454.1 3.9 copy.38
  458.1 3.4 all-to-all-done.2
  461.4 0.5 broadcast.64
  461.9 1.0 reduce.1
  462.9 0.1 reshape.138
  463.1 0.0 copy-start.1
  463.1 3.3 fusion
  466.4 0.2 copy-done.1
  466.5 3.5 fusion.18
  470.0 1.7 copy.43
  471.7 1.5 concatenate.6
  473.2 0.1 convert_element_type.92
  473.3 1.5 pad_maximum_fusion
  474.8 17.4 %all_to_all.25 = bf16[8,2,16640]{2,1,0:T(2,128)(2,1)S(1)} all-to-all(bf16[8,2,16640]{2,1,0:T(2,128)(2,1)S(1)} %pad_maximum_fusion), channel_id=1, replica_groups=mesh['groups'=2,'seq'=16,'qset'=8] {'qset'}, dimensions={0} | all-to-all | bytes 1064960 | tf_op jit(solution)/shard_map/all_to_all | solution.py:43
  492.2 0.5 convert_reduce_fusion.1
  492.7 0.1 reshape.131
  492.8 0.1 copy.44
  492.9 0.2 div.27
  493.1 0.2 div.28
  493.3 0.1 reshape.130
  493.4 0.0 copy-done
  493.4 0.4 convolution_convert_fusion
  493.9 1.1 copy.53
  495.0 9.8 %all-to-all-start.4 = ((bf16[16,256,128]{1,2,0:T(8,128)(2,1)}), bf16[16,256,128]{1,2,0:T(8,128)(2,1)S(1)}, u32[]{:S(2)}, u32[]{:S(2)}) async-start(bf16[16,256,128]{1,2,0:T(8,128)(2,1)} %bitcast.57), calls=%async_computation.4 | async-start | bytes 2097152 | tf_op jit(solution)/shard_map/all_to_all | solution.py:43
  504.8 28.0 %all-to-all-done.4 = bf16[16,256,128]{1,2,0:T(8,128)(2,1)S(1)} async-done(((bf16[16,256,128]{1,2,0:T(8,128)(2,1)}), bf16[16,256,128]{1,2,0:T(8,128)(2,1)S(1)}, u32[]{:S(2)}, u32[]{:S(2)}) %all-to-all-start.4) | async-done | bytes 1048608 | tf_op jit(solution)/shard_map/all_to_all | solution.py:43
  532.7 0.1 convert_reduce_fusion
  532.9 1.5 add_convert_fusion
  (16 shorter events, 0.2 us)
Async XLA Ops:
  0.0 493.4 %copy-start = (bf16[256,4096]{1,0:T(8,128)(2,1)S(1)}, bf16[256,4096]{1,0:T(8,128)(2,1)}, u32[]{:S(2)}) copy-start(bf16[256,4096]{1,0:T(8,128)(2,1)} %param.14) | copy-start | bytes 6291460
  0.0 4.1 copy-start.3
  4.5 18.1 %copy-start.4 = (bf16[4096]{0:T(1024)(128)(2,1)S(1)}, bf16[4096]{0:T(1024)(128)(2,1)}, u32[]{:S(2)}) copy-start(bf16[4096]{0:T(1024)(128)(2,1)} %param.9) | copy-start | bytes 24580
  4.5 18.1 %copy-start.2 = (bf16[1,1,128,4096]{3,2,1,0:T(8,128)(2,1)S(1)}, bf16[1,1,128,4096]{3,2,1,0:T(8,128)(2,1)}, u32[]{:S(2)}) copy-start(bf16[1,1,128,4096]{3,2,1,0:T(8,128)(2,1)} %param.8) | copy-start | bytes 3145732
  9.0 25.9 %all-to-all-start.1 = ((bf16[8,2,16384]{2,1,0:T(2,128)(2,1)}), bf16[8,2,16384]{2,1,0:T(2,128)(2,1)}, u32[]{:S(2)}, u32[]{:S(2)}) async-start(bf16[8,2,16384]{2,1,0:T(2,128)(2,1)} %reshape.135), calls=%async_computation.1 | async-start | bytes 1048576 | tf_op jit(solution)/shard_map/all_to_all | solution.py:15
  40.8 17.0 %copy-start.5 = (s32[8,16,1]{1,2,0:T(1,128)S(1)}, s32[8,16,1]{1,2,0:T(1,128)}, u32[]{:S(2)}) copy-start(s32[8,16,1]{1,2,0:T(1,128)} %param.15) | copy-start | bytes 1540
  40.8 380.4 %all-to-all-start = ((bf16[16,1,128,4096]{3,2,1,0:T(8,128)(2,1)}), bf16[16,1,128,4096]{3,2,1,0:T(8,128)(2,1)}, u32[]{:S(2)}, u32[]{:S(2)}) async-start(bf16[16,1,128,4096]{3,2,1,0:T(8,128)(2,1)} %stack.3), calls=%async_computation | async-start | bytes 33554432 | tf_op jit(solution)/shard_map/all_to_all | solution.py:82
  450.3 11.1 %all-to-all-start.2 = ((f32[8,1,4096]{2,1,0:T(1,128)}), f32[8,1,4096]{2,1,0:T(1,128)S(1)}, u32[]{:S(2)}, u32[]{:S(2)}) async-start(f32[8,1,4096]{2,1,0:T(1,128)} %reshape.137), calls=%async_computation.2 | async-start | bytes 262144 | tf_op jit(solution)/shard_map/all_to_all | solution.py:15
  463.1 3.5 copy-start.1
  495.0 37.7 %all-to-all-start.4 = ((bf16[16,256,128]{1,2,0:T(8,128)(2,1)}), bf16[16,256,128]{1,2,0:T(8,128)(2,1)S(1)}, u32[]{:S(2)}, u32[]{:S(2)}) async-start(bf16[16,256,128]{1,2,0:T(8,128)(2,1)} %bitcast.57), calls=%async_computation.4 | async-start | bytes 2097152 | tf_op jit(solution)/shard_map/all_to_all | solution.py:43
